TPU v7x, 32 devices: a whole 2x2x4 slice. The times are simulated.
32 devices in a mesh: pipe: 2 (over x), tensor: 4 (over y, core), seq: 4 (over z).
Axes of the slice: x: 2, y: 2, z: 4, core: 2. Of those that a mesh axis runs over, the one named last changes fastest.
Arguments:
- tokens: bfloat16 [2, 512, 2560], P(None, 'seq', 'tensor'), may hold values from -6 to 6
- prenorm_gain: float32 [2, 2560], P('pipe'), may hold values from 0.5 to 1.5
- gate_weight: bfloat16 [2, 2560, 5120], P('pipe', None, 'tensor'), may hold values from -0.125 to 0.125
- inner_weight: bfloat16 [2, 2560, 5120], P('pipe', None, 'tensor'), may hold values from -0.125 to 0.125
- state_weight: bfloat16 [2, 2560, 256], P('pipe'), may hold values from -0.125 to 0.125
- step_weight: bfloat16 [2, 2560, 80], P('pipe', None, 'tensor'), may hold values from -0.125 to 0.125
- inner_taps: float32 [2, 5, 5120], P('pipe', None, 'tensor'), may hold values from -3 to 3
- state_taps: float32 [2, 5, 256], P('pipe'), may hold values from -3 to 3
- step_bias: float32 [2, 80], P('pipe', 'tensor'), may hold values from -5 to -2
- decay_rate: float32 [2, 80], P('pipe', 'tensor'), may hold values from 0.001953125 to 1
- skip_scale: float32 [2, 80], P('pipe', 'tensor'), may hold values from 0.5 to 1.5
- inner_gain: float32 [2, 5120], P('pipe', 'tensor'), may hold values from 0.5 to 1.5
- out_weight: bfloat16 [2, 5120, 2560], P('pipe', 'tensor'), may hold values from -0.078125 to 0.078125
Outputs:
- layer_outputs: bfloat16 [2, 2, 512, 2560], P('pipe', None, 'seq', 'tensor')
All inputs are finite; a program needn't handle non-finite values.
Results may differ from a plain program's by a relative error of at most 0.019.
Values may be sent and summed in bfloat16 or wider, within the bound.
A program may use at most 64 MiB of HBM per device.

v0:
```python
import jax
import jax.numpy as jnp
from jax import lax
from jax.sharding import PartitionSpec as P

BLOCK = 128
INNER = 5120
EPS = 1e-05


def shifted(value, axis, steps):
    count = lax.axis_size(axis)
    first, last = (max(0, -steps), min(count, count - steps))
    return lax.ppermute(value, axis, [(source, source + steps) for source in range(first, last)])


def prefix(array, axis, join, neutral):
    place = lax.axis_index(axis)
    gathered = jax.tree.map(
        lambda a, kind: lax.all_gather(a.astype(kind), axis), array, (jnp.bfloat16, jnp.bfloat16)
    )
    state = jax.tree.map(lambda a, e: jnp.zeros_like(a) + jnp.asarray(e, a.dtype), array, neutral)

    def one(hop, state):
        return join(
            state,
            jax.tree.map(
                lambda a, own: lax.dynamic_index_in_dim(a, hop, 0, False).astype(own.dtype),
                gathered,
                array,
            ),
        )

    return lax.fori_loop(0, place, one, state)


def causal_taps(rim, values, taps):
    width = taps.shape[0] - 1
    length = values.shape[0]
    padded = jnp.concatenate([rim, values], axis=0).astype(jnp.float32)
    total = jnp.broadcast_to(taps[width][None, :], (length, values.shape[1]))
    for index in range(width):
        total = total + taps[index][None, :] * padded[index : index + length]
    return jax.nn.silu(total).astype(jnp.bfloat16)


def fold_states(carried, items):
    decay_acc, state_acc = carried
    decay, state = items
    return ((decay_acc * decay, state_acc * decay[:, None, None] + state), (decay_acc, state_acc))


def combine_states(earlier, later):
    return (earlier[0] * later[0], earlier[1] * later[0][:, None, None] + later[1])


def mixer(current, weights):
    (
        prenorm,
        gate_weight,
        inner_weight,
        state_weight,
        step_weight,
        inner_taps,
        state_taps,
        step_bias,
        decay_rate,
        skip_scale,
        inner_gain,
        out_weight,
    ) = weights
    rows = current.shape[0]
    widened = current.astype(jnp.float32)
    normed_in = (
        widened * lax.rsqrt(jnp.mean(widened * widened, axis=1, keepdims=True) + EPS) * prenorm
    ).astype(jnp.bfloat16)
    gate_raw = jnp.dot(normed_in, gate_weight, preferred_element_type=jnp.float32).astype(
        jnp.bfloat16
    )
    inner_raw = jnp.dot(normed_in, inner_weight, preferred_element_type=jnp.float32).astype(
        jnp.bfloat16
    )
    state_raw = jnp.dot(normed_in, state_weight, preferred_element_type=jnp.float32).astype(
        jnp.bfloat16
    )
    step_raw = jnp.dot(normed_in, step_weight, preferred_element_type=jnp.float32)
    inner_width = inner_raw.shape[1]
    reach = inner_taps.shape[0] - 2
    rim = shifted(
        jnp.concatenate([inner_raw[rows - reach :], state_raw[rows - reach :]], axis=1), "seq", 1
    )
    inner_conv = causal_taps(rim[:, :inner_width], inner_raw, inner_taps)
    state_conv = causal_taps(rim[:, inner_width:], state_raw, state_taps)
    heads = step_bias.shape[0]
    head_size = inner_width // heads
    state_size = state_raw.shape[1] // 2
    blocks = rows // BLOCK
    step_size = jax.nn.softplus(step_raw + step_bias)
    step_blocks = step_size.reshape(blocks, BLOCK, heads)
    cumulative = jnp.cumsum(-step_blocks * decay_rate, axis=1)
    inner_blocks = inner_conv.reshape(blocks, BLOCK, heads, head_size)
    input_blocks = state_conv[:, :state_size].reshape(blocks, BLOCK, state_size)
    output_blocks = state_conv[:, state_size:].reshape(blocks, BLOCK, state_size)
    weighting = jnp.exp(cumulative[:, -1:, :] - cumulative) * step_blocks
    weighted = (inner_blocks.astype(jnp.float32) * weighting[..., None]).astype(jnp.bfloat16)
    states = jnp.einsum(
        "bshp,bsn->bhpn", weighted, input_blocks, preferred_element_type=jnp.float32
    )
    decays = jnp.exp(cumulative[:, -1, :])
    start = (
        jnp.ones((heads,), jnp.float32),
        jnp.zeros((heads, head_size, state_size), jnp.float32),
    )
    (device_decay, device_state), (prior_decay, prior_state) = lax.scan(
        fold_states, start, (decays, states)
    )
    entry_decay, entry_state = prefix(
        (device_decay, device_state),
        "seq",
        combine_states,
        (jnp.ones_like(device_decay), jnp.zeros_like(device_state)),
    )
    scores = jnp.einsum(
        "bqn,bsn->bqs", output_blocks, input_blocks, preferred_element_type=jnp.float32
    )
    by_head = jnp.transpose(cumulative, (0, 2, 1))
    later = lax.broadcasted_iota(jnp.int32, (BLOCK, BLOCK), 0) >= lax.broadcasted_iota(
        jnp.int32, (BLOCK, BLOCK), 1
    )
    decay = jnp.exp(jnp.where(later, by_head[:, :, :, None] - by_head[:, :, None, :], -jnp.inf))
    mixing = (
        scores[:, None] * decay * jnp.transpose(step_blocks, (0, 2, 1))[:, :, None, :]
    ).astype(jnp.bfloat16)
    inside = jnp.einsum("bhqs,bshp->bqhp", mixing, inner_blocks, preferred_element_type=jnp.float32)
    entering = prior_state + prior_decay[:, :, None, None] * entry_state[None]
    across = jnp.exp(cumulative)[..., None] * jnp.einsum(
        "bqn,bhpn->bqhp",
        output_blocks.astype(jnp.float32),
        entering,
        precision=lax.Precision.HIGHEST,
    )
    mixed = inside + across + skip_scale[None, None, :, None] * inner_blocks.astype(jnp.float32)
    mixed = mixed.reshape(rows, inner_width)
    gated = mixed * jax.nn.silu(gate_raw.astype(jnp.float32))
    squares = lax.psum(jnp.sum(gated * gated, axis=1), "tensor")
    normed = (gated * lax.rsqrt(squares / INNER + EPS)[:, None] * inner_gain).astype(jnp.bfloat16)
    return jnp.dot(normed, out_weight, preferred_element_type=jnp.float32)


def shards(
    tokens,
    prenorm_gain,
    gate_weight,
    inner_weight,
    state_weight,
    step_weight,
    inner_taps,
    state_taps,
    step_bias,
    decay_rate,
    skip_scale,
    inner_gain,
    out_weight,
):
    weights = (
        prenorm_gain[0],
        gate_weight[0],
        inner_weight[0],
        state_weight[0],
        step_weight[0],
        inner_taps[0],
        state_taps[0],
        step_bias[0],
        decay_rate[0],
        skip_scale[0],
        inner_gain[0],
        out_weight[0],
    )
    sections = lax.axis_size("pipe")
    section = lax.axis_index("pipe")
    share = lax.axis_size("tensor")
    member = lax.axis_index("tensor")
    all_tokens = lax.all_gather(tokens, "tensor", axis=2, tiled=True)
    micro_count, rows, width = all_tokens.shape
    narrow = width // share
    outputs = jnp.zeros((micro_count, rows, narrow), jnp.bfloat16)
    carried = None
    rounds = micro_count + sections - 1
    for turn in range(rounds):
        fresh = all_tokens[min(turn, micro_count - 1)]
        if turn == 0:
            current = fresh
        else:
            incoming = lax.all_gather(carried, "tensor", axis=1, tiled=True)
            current = jnp.where(section == 0, fresh, incoming)
        term = mixer(current, weights)
        summed = lax.psum_scatter(
            term.astype(jnp.bfloat16), "tensor", scatter_dimension=1, tiled=True
        ).astype(jnp.float32)
        base = lax.dynamic_slice_in_dim(current, member * narrow, narrow, 1)
        own = (base.astype(jnp.float32) + summed).astype(jnp.bfloat16)
        micro = turn - section
        valid = jnp.logical_and(micro >= 0, micro < micro_count)
        position = jnp.clip(micro, 0, micro_count - 1)
        previous = lax.dynamic_index_in_dim(outputs, position, 0, keepdims=False)
        outputs = lax.dynamic_update_index_in_dim(
            outputs, jnp.where(valid, own, previous), position, 0
        )
        if turn + 1 < rounds:
            carried = shifted(own, "pipe", 1)
    return outputs[None]


def solution(mesh):
    placed = (
        P(None, "seq", "tensor"),
        P("pipe", None),
        P("pipe", None, "tensor"),
        P("pipe", None, "tensor"),
        P("pipe", None, None),
        P("pipe", None, "tensor"),
        P("pipe", None, "tensor"),
        P("pipe", None, None),
        P("pipe", "tensor"),
        P("pipe", "tensor"),
        P("pipe", "tensor"),
        P("pipe", "tensor"),
        P("pipe", "tensor", None),
    )
    return jax.shard_map(
        shards,
        mesh=mesh,
        in_specs=placed,
        out_specs=P("pipe", None, "seq", "tensor"),
        check_vma=False,
    )
```

profile of v0, /device:TPU:0, one launch (start us, length us, event | category | flops | bytes accessed | tf_op | source)
XLA Modules:
  0.0 362.3 jit_solution(9276554146936817338)
XLA Ops:
  9.6 20.2 %all-gather.11.cloned.1.call-done = bf16[2,128,2560]{2,1,0:T(8,128)(2,1)} async-done(((bf16[2,128,640]{2,1,0:T(8,128)(2,1)}), bf16[2,128,2560]{2,1,0:T(8,128)(2,1)}) %all-gather.11.cloned.1.call-update) | async-done | bytes 1310736 | tf_op jit(solution)/shard_map/all_gather | solution.py:183
  29.8 1.4 fusion.54
  31.2 1.5 compare_select_fusion.2
  33.8 3.9 %fusion.27 = bf16[128,1280]{1,0:T(8,128)(2,1)S(1)} fusion(bf16[1,2560,1280]{2,1,0:T(8,128)(2,1)} %param.22, f32[2560]{0:T(1024)S(1)} %reduce.3, f32[128]{0:T(128)S(1)} %add_rsqrt_fusion.5, bf16[2,128,2560]{2,1,0:T(8,128)(2,1)S(1)} %copy-done.1), kind=kOutput, calls=%fused_computation.27 | convolution fusion | flops 840335360 | bytes 7549440 | tf_op jit(solution)/shard_map/dot_general | solution.py:80
  39.1 3.4 collective-permute-start
  42.6 1.1 copy.73
  45.1 1.2 multiply_convert_fusion.13
  46.3 1.2 copy.74
  48.8 11.7 %all-gather = bf16[4,1,20]{2,1,0:T(2,128)(2,1)S(1)} all-gather(bf16[1,1,20]{2,1,0:T(2,128)(2,1)S(1)} %copy-done.25), channel_id=2, replica_groups=mesh['pipe'=2,'tensor'=4,'seq'=4] {'seq'}, dimensions={0}, use_global_device_ids=true | all-gather | bytes 200 | tf_op jit(solution)/shard_map/all_gather | solution.py:20
  62.6 19.5 %all-gather.13.cloned.1.call-done = bf16[80,64,128]{2,1,0:T(8,128)(2,1)} async-done(((bf16[20,64,128]{2,1,0:T(8,128)(2,1)}), bf16[80,64,128]{2,1,0:T(8,128)(2,1)}) %all-gather.13.cloned.1.call-update) | async-done | bytes 1310736 | tf_op jit(solution)/shard_map/all_gather | solution.py:20
  84.1 1.1 copy.76
  85.2 5.0 %multiply_reduce_fusion.2 = (f32[128]{0:T(128)S(1)}, f32[128,1280]{1,0:T(8,128)}) fusion(f32[128,1280]{1,0:T(8,128)} %copy.76, bf16[1,2560,1280]{2,1,0:T(8,128)(2,1)} %param.21, f32[2560]{0:T(1024)S(1)} %reduce.3, f32[128]{0:T(128)S(1)} %copy-done.22, bf16[2,128,2560]{2,1,0:T(8,128)(2,1)S(1)} %copy-done.1), kind=kOutput, calls=%fused_computation.132 | convolution fusion | flops 841645952 | bytes 8532992 | tf_op jit(solution)/shard_map/dot_general | solution.py:77
  90.1 5.8 %psum.21 = f32[128]{0:T(128)S(1)} all-reduce(f32[128]{0:T(128)S(1)} %get-tuple-element.269), channel_id=1, replica_groups=mesh['pipe'=2,'tensor'=4,'seq'=4] {'tensor'}, use_global_device_ids=true, to_apply=%region_5.6 | all-reduce | flops 128 | bytes 1024 | tf_op jit(solution)/shard_map/psum | solution.py:145
  96.0 4.2 %fusion.18 = bf16[128,2560]{1,0:T(8,128)(2,1)S(1)} fusion(bf16[1,1280,2560]{2,1,0:T(8,128)(2,1)} %param.31, f32[128,1280]{1,0:T(8,128)} %get-tuple-element.270, f32[1280]{0:T(1024)S(1)} %reduce.7, f32[128]{0:T(128)S(1)} %add_rsqrt_fusion.4), kind=kOutput, calls=%fused_computation.24 | convolution fusion | flops 839680000 | bytes 7869952 | tf_op jit(solution)/shard_map/dot_general | solution.py:147
  100.1 1.1 copy.95
  101.3 25.3 %reduce-scatter.10.cloned.1.call-done = bf16[640,128]{1,0:T(8,128)(2,1)} async-done(((bf16[2560,128]{1,0:T(8,128)(2,1)}), bf16[640,128]{1,0:T(8,128)(2,1)}) %reduce-scatter.10.cloned.1.call-update) | async-done | bytes 163856
  126.6 1.1 copy.96
  129.2 3.4 collective-permute-start.1
  132.6 3.6 collective-permute-done.1
  136.2 6.9 %all_gather.36 = bf16[128,2560]{1,0:T(8,128)(2,1)S(1)} all-gather(bf16[128,640]{1,0:T(8,128)(2,1)S(1)} %collective-permute-done.1), channel_id=1, replica_groups=mesh['pipe'=2,'tensor'=4,'seq'=4] {'tensor'}, dimensions={1}, use_global_device_ids=true | all-gather | bytes 819200 | tf_op jit(solution)/shard_map/all_gather | solution.py:194
  143.9 4.0 %fusion.30 = bf16[128,1280]{1,0:T(8,128)(2,1)S(1)} fusion(bf16[1,2560,1280]{2,1,0:T(8,128)(2,1)} %param.22, bf16[128,2560]{1,0:T(8,128)(2,1)S(1)} %get-tuple-element.247, f32[2560]{0:T(1024)S(1)} %reduce.3, f32[128]{0:T(128)S(1)} %add_rsqrt_fusion.3), kind=kOutput, calls=%fused_computation.28 | convolution fusion | flops 840335360 | bytes 7547392 | tf_op jit(solution)/shard_map/dot_general | solution.py:80
  149.9 4.0 %collective-permute-start.2 = (bf16[3,1536]{1,0:T(4,128)(2,1)}, bf16[3,1536]{1,0:T(4,128)(2,1)}, u32[]{:S(2)}, u32[]{:S(2)}) collective-permute-start(bf16[3,1536]{1,0:T(4,128)(2,1)} %pad_maximum_fusion.1), channel_id=1, source_target_pairs={{0,1},{1,2},{2,3},{4,5},{5,6},{6,7},{8,9},{9,10},{10,11},{12,13},{... | collective-permute-start | bytes 27656 | tf_op jit(solution)/shard_map/ppermute | solution.py:14
  154.1 1.1 copy.82
  157.8 1.2 multiply_convert_fusion.10
  159.0 1.2 copy.83
  161.2 11.7 %all-gather.2 = bf16[4,1,20]{2,1,0:T(2,128)(2,1)S(1)} all-gather(bf16[1,1,20]{2,1,0:T(2,128)(2,1)S(1)} %copy-done.26), channel_id=4, replica_groups=mesh['pipe'=2,'tensor'=4,'seq'=4] {'seq'}, dimensions={0}, use_global_device_ids=true | all-gather | bytes 200 | tf_op jit(solution)/shard_map/all_gather | solution.py:20
  175.0 21.2 %all-gather.15.cloned.1.call-done = bf16[80,64,128]{2,1,0:T(8,128)(2,1)} async-done(((bf16[20,64,128]{2,1,0:T(8,128)(2,1)}), bf16[80,64,128]{2,1,0:T(8,128)(2,1)}) %all-gather.15.cloned.1.call-update) | async-done | bytes 1310736 | tf_op jit(solution)/shard_map/all_gather | solution.py:20
  197.5 1.5 fusion.76
  199.1 2.2 copy.85
  201.3 5.0 %multiply_reduce_fusion.1 = (f32[128]{0:T(128)S(1)}, f32[128,1280]{1,0:T(8,128)}) fusion(f32[128,1280]{1,0:T(8,128)} %copy.85, bf16[1,2560,1280]{2,1,0:T(8,128)(2,1)} %param.21, bf16[128,2560]{1,0:T(8,128)(2,1)S(1)} %copy-done.5, f32[2560]{0:T(1024)S(1)} %reduce.3, f32[128]{0:T(128)S(1)} %copy-done.24), kind=kOutput, calls=%fused_computation.123 | convolution fusion | flops 841645952 | bytes 8530944 | tf_op jit(solution)/shard_map/dot_general | solution.py:77
  206.3 5.8 %psum.22 = f32[128]{0:T(128)S(1)} all-reduce(f32[128]{0:T(128)S(1)} %get-tuple-element.271), channel_id=1, replica_groups=mesh['pipe'=2,'tensor'=4,'seq'=4] {'tensor'}, use_global_device_ids=true, to_apply=%region_12.13 | all-reduce | flops 128 | bytes 1024 | tf_op jit(solution)/shard_map/psum | solution.py:145
  212.1 5.0 %fusion.21 = bf16[128,2560]{1,0:T(8,128)(2,1)} fusion(bf16[1,1280,2560]{2,1,0:T(8,128)(2,1)} %param.31, f32[128,1280]{1,0:T(8,128)} %get-tuple-element.272, f32[128]{0:T(128)S(1)} %add_rsqrt_fusion.2, f32[1280]{0:T(1024)S(1)} %reduce.7), kind=kOutput, calls=%fused_computation.25 | convolution fusion | flops 839680000 | bytes 7869952 | tf_op jit(solution)/shard_map/dot_general | solution.py:147
  217.1 2.2 copy.97
  220.3 24.4 %reduce-scatter.12.cloned.1.call-done = bf16[640,128]{1,0:T(8,128)(2,1)} async-done(((bf16[2560,128]{1,0:T(8,128)(2,1)}), bf16[640,128]{1,0:T(8,128)(2,1)}) %reduce-scatter.12.cloned.1.call-update) | async-done | bytes 163856
  244.7 1.7 copy.98
  246.4 1.6 bitcast_dynamic-update-slice_fusion
  248.1 3.3 collective-permute-start.3
  251.5 3.3 collective-permute-done.3
  254.8 6.9 %all_gather.39 = bf16[128,2560]{1,0:T(8,128)(2,1)S(1)} all-gather(bf16[128,640]{1,0:T(8,128)(2,1)S(1)} %collective-permute-done.3), channel_id=1, replica_groups=mesh['pipe'=2,'tensor'=4,'seq'=4] {'tensor'}, dimensions={1}, use_global_device_ids=true | all-gather | bytes 819200 | tf_op jit(solution)/shard_map/all_gather | solution.py:194
  262.4 4.0 %fusion.33 = bf16[128,1280]{1,0:T(8,128)(2,1)S(1)} fusion(bf16[1,2560,1280]{2,1,0:T(8,128)(2,1)} %param.22, bf16[128,2560]{1,0:T(8,128)(2,1)S(1)} %get-tuple-element.241, f32[128]{0:T(128)S(1)} %add_rsqrt_fusion.1, f32[2560]{0:T(1024)S(1)} %reduce.3), kind=kOutput, calls=%fused_computation.29 | convolution fusion | flops 840335360 | bytes 7547392 | tf_op jit(solution)/shard_map/dot_general | solution.py:80
  267.4 3.4 collective-permute-start.4
  274.1 11.7 %all-gather.4 = bf16[4,1,20]{2,1,0:T(2,128)(2,1)S(1)} all-gather(bf16[1,1,20]{2,1,0:T(2,128)(2,1)S(1)} %get-tuple-element.253), channel_id=6, replica_groups=mesh['pipe'=2,'tensor'=4,'seq'=4] {'seq'}, dimensions={0}, use_global_device_ids=true | all-gather | bytes 200 | tf_op jit(solution)/shard_map/all_gather | solution.py:20
  287.1 22.4 %all-gather.17.cloned.1.call-done = bf16[80,64,128]{2,1,0:T(8,128)(2,1)} async-done(((bf16[20,64,128]{2,1,0:T(8,128)(2,1)}), bf16[80,64,128]{2,1,0:T(8,128)(2,1)}) %all-gather.17.cloned.1.call-update) | async-done | bytes 1310736 | tf_op jit(solution)/shard_map/all_gather | solution.py:20
  312.3 4.9 %multiply_reduce_fusion = (f32[128]{0:T(128)S(1)}, f32[128,1280]{1,0:T(8,128)}) fusion(f32[128,1280]{1,0:T(8,128)S(1)} %copy.94, bf16[1,2560,1280]{2,1,0:T(8,128)(2,1)} %param.21, bf16[128,2560]{1,0:T(8,128)(2,1)S(1)} %copy-done.3, f32[128]{0:T(128)S(1)} %copy-done.20, f32[2560]{0:T(1024)S(1)} %reduce.3), kind=kOutput, calls=%fused_computation.114 | convolution fusion | flops 841645952 | bytes 8530944 | tf_op jit(solution)/shard_map/dot_general | solution.py:77
  317.2 5.8 %psum.23 = f32[128]{0:T(128)S(1)} all-reduce(f32[128]{0:T(128)S(1)} %get-tuple-element.273), channel_id=1, replica_groups=mesh['pipe'=2,'tensor'=4,'seq'=4] {'tensor'}, use_global_device_ids=true, to_apply=%region_19.20 | all-reduce | flops 128 | bytes 1024 | tf_op jit(solution)/shard_map/psum | solution.py:145
  323.0 4.2 %fusion.24 = bf16[128,2560]{1,0:T(8,128)(2,1)S(1)} fusion(bf16[1,1280,2560]{2,1,0:T(8,128)(2,1)} %param.31, f32[128,1280]{1,0:T(8,128)} %get-tuple-element.274, f32[128]{0:T(128)S(1)} %add_rsqrt_fusion, f32[1280]{0:T(1024)S(1)} %reduce.7), kind=kOutput, calls=%fused_computation.26 | convolution fusion | flops 839680000 | bytes 7869952 | tf_op jit(solution)/shard_map/dot_general | solution.py:147
  327.2 1.1 copy.99
  329.1 24.6 %reduce-scatter.14.cloned.1.call-done = bf16[640,128]{1,0:T(8,128)(2,1)} async-done(((bf16[2560,128]{1,0:T(8,128)(2,1)}), bf16[640,128]{1,0:T(8,128)(2,1)}) %reduce-scatter.14.cloned.1.call-update) | async-done | bytes 163856
  (192 shorter events, 36.0 us)
Async XLA Ops:
  6.5 31.3 %copy-start = (bf16[1,2560,256]{2,1,0:T(8,128)(2,1)S(1)}, bf16[1,2560,256]{2,1,0:T(8,128)(2,1)}, u32[]{:S(2)}) copy-start(bf16[1,2560,256]{2,1,0:T(8,128)(2,1)} %param.23) | copy-start | bytes 3932164
  6.5 26.2 %copy-start.18 = (f32[1,20]{1,0:T(1,128)S(1)}, f32[1,20]{1,0:T(1,128)}, u32[]{:S(2)}) copy-start(f32[1,20]{1,0:T(1,128)} %param.28) | copy-start | bytes 244
  6.5 23.3 %all-gather.11.cloned.1.call-start = ((), (), s32[]{:S(2)}) async-start(), calls=%async_computation.3 | async-start | bytes 1638400 | tf_op jit(solution)/shard_map/all_gather | solution.py:183
  7.3 74.9 %all-gather.13.cloned.1.call-start = ((), (), s32[]{:S(2)}) async-start(), calls=%async_computation.4 | async-start | bytes 1638400 | tf_op jit(solution)/shard_map/all_gather | solution.py:20
  29.8 4.0 %copy-start.1 = (bf16[2,128,2560]{2,1,0:T(8,128)(2,1)S(1)}, bf16[2,128,2560]{2,1,0:T(8,128)(2,1)}, u32[]{:S(2)}) copy-start(bf16[2,128,2560]{2,1,0:T(8,128)(2,1)} %all-gather.11.cloned.1.call-done) | copy-start | bytes 3932164
  31.2 6.6 %copy-start.21 = (f32[128]{0:T(128)}, f32[128]{0:T(128)S(1)}, u32[]{:S(2)}) copy-start(f32[128]{0:T(128)S(1)} %add_rsqrt_fusion.5) | copy-start | bytes 1540
  37.8 0.7 copy-start.11
  39.1 5.0 %collective-permute-start = (bf16[3,1536]{1,0:T(4,128)(2,1)}, bf16[3,1536]{1,0:T(4,128)(2,1)S(1)}, u32[]{:S(2)}, u32[]{:S(2)}) collective-permute-start(bf16[3,1536]{1,0:T(4,128)(2,1)} %pad_maximum_fusion), channel_id=1, source_target_pairs={{0,1},{1,2},{2,3},{4,5},{5,6},{6,7},{8,9},{9,10},{10,11},{12,13},{... | collective-permute-start | bytes 27656 | tf_op jit(solution)/shard_map/ppermute | solution.py:14
  43.7 1.4 copy-start.9
  46.3 2.4 copy-start.17
  46.3 2.4 copy-start.25
  48.7 78.0 %reduce-scatter.10.cloned.1.call-start = ((), (), s32[]{:S(2)}) async-start(), calls=%async_computation.7 | async-start | bytes 819200
  82.2 1.1 copy-start.12
  82.2 1.2 copy-start.15
  82.2 1.2 copy-start.31
  84.1 1.1 copy-start.22
  101.2 26.5 %slice-start = ((bf16[2,128,2560]{2,1,0:T(8,128)(2,1)}), bf16[1,128,2560]{2,1,0:T(8,128)(2,1)S(1)}, s32[]{:S(2)}) async-start(bf16[2,128,2560]{2,1,0:T(8,128)(2,1)} %all-gather.11.cloned.1.call-done), calls=%async_computation.10 | async-start | bytes 1310720 | tf_op jit(solution)/shard_map/slice | solution.py:190
  101.2 95.0 %all-gather.15.cloned.1.call-start = ((), (), s32[]{:S(2)}) async-start(), calls=%async_computation.5 | async-start | bytes 1638400 | tf_op jit(solution)/shard_map/all_gather | solution.py:20
  128.5 0.7 copy-start.6
  129.2 7.0 %collective-permute-start.1 = (bf16[128,640]{1,0:T(8,128)(2,1)}, bf16[128,640]{1,0:T(8,128)(2,1)S(1)}, u32[]{:S(2)}, u32[]{:S(2)}) collective-permute-start(bf16[128,640]{1,0:T(8,128)(2,1)} %get-tuple-element.249), channel_id=1, source_target_pairs={{0,16},{1,17},{2,18},{3,19},{4,20},{5,21},{6,22},{7,23},{8,24},{9,... | collective-permute-start | bytes 491528 | tf_op jit(solution)/shard_map/ppermute | solution.py:14
  143.4 4.5 %copy-start.4 = (bf16[128,2560]{1,0:T(8,128)(2,1)}, bf16[128,2560]{1,0:T(8,128)(2,1)S(1)}, u32[]{:S(2)}) copy-start(bf16[128,2560]{1,0:T(8,128)(2,1)S(1)} %get-tuple-element.247) | copy-start | bytes 1966084
  143.4 4.5 %copy-start.23 = (f32[128]{0:T(128)}, f32[128]{0:T(128)S(1)}, u32[]{:S(2)}) copy-start(f32[128]{0:T(128)S(1)} %add_rsqrt_fusion.3) | copy-start | bytes 1540
  143.9 4.1 %copy-start.27 = (bf16[1,2560,20]{1,2,0:T(8,128)(2,1)S(1)}, bf16[1,2560,20]{1,2,0:T(8,128)(2,1)}, u32[]{:S(2)}) copy-start(bf16[1,2560,20]{1,2,0:T(8,128)(2,1)} %param.24) | copy-start | bytes 307204
  143.9 4.1 %copy-start.29 = (f32[1,20]{1,0:T(1,128)S(1)}, f32[1,20]{1,0:T(1,128)}, u32[]{:S(2)}) copy-start(f32[1,20]{1,0:T(1,128)} %param.27) | copy-start | bytes 244
  147.9 6.1 %copy-start.10 = (bf16[128,1280]{1,0:T(8,128)(2,1)}, bf16[128,1280]{1,0:T(8,128)(2,1)S(1)}, u32[]{:S(2)}) copy-start(bf16[128,1280]{1,0:T(8,128)(2,1)S(1)} %fusion.30) | copy-start | bytes 983044
  149.9 5.2 %collective-permute-start.2 = (bf16[3,1536]{1,0:T(4,128)(2,1)}, bf16[3,1536]{1,0:T(4,128)(2,1)}, u32[]{:S(2)}, u32[]{:S(2)}) collective-permute-start(bf16[3,1536]{1,0:T(4,128)(2,1)} %pad_maximum_fusion.1), channel_id=1, source_target_pairs={{0,1},{1,2},{2,3},{4,5},{5,6},{6,7},{8,9},{9,10},{10,11},{12,13},{... | collective-permute-start | bytes 27656 | tf_op jit(solution)/shard_map/ppermute | solution.py:14
  155.1 2.6 copy-start.8
  159.0 2.2 copy-start.26
  161.2 83.6 %reduce-scatter.12.cloned.1.call-start = ((), (), s32[]{:S(2)}) async-start(), calls=%async_computation.8 | async-start | bytes 819200
  196.4 1.1 copy-start.13
  196.4 1.2 copy-start.16
  196.4 1.2 copy-start.32
  199.1 2.2 copy-start.5
  199.1 2.2 copy-start.24
  219.3 90.2 %all-gather.17.cloned.1.call-start = ((), (), s32[]{:S(2)}) async-start(), calls=%async_computation.6 | async-start | bytes 1638400 | tf_op jit(solution)/shard_map/all_gather | solution.py:20
  248.1 6.7 %collective-permute-start.3 = (bf16[128,640]{1,0:T(8,128)(2,1)S(1)}, bf16[128,640]{1,0:T(8,128)(2,1)S(1)}, u32[]{:S(2)}, u32[]{:S(2)}) collective-permute-start(bf16[128,640]{1,0:T(8,128)(2,1)S(1)} %get-tuple-element.243), channel_id=1, source_target_pairs={{0,16},{1,17},{2,18},{3,19},{4,20},{5,21},{6,22},{7,23},{8,24},{9,... | collective-permute-start | bytes 491528 | tf_op jit(solution)/shard_map/ppermute | solution.py:14
  262.0 4.5 %copy-start.2 = (bf16[128,2560]{1,0:T(8,128)(2,1)}, bf16[128,2560]{1,0:T(8,128)(2,1)S(1)}, u32[]{:S(2)}) copy-start(bf16[128,2560]{1,0:T(8,128)(2,1)S(1)} %get-tuple-element.241) | copy-start | bytes 1966084
  262.0 4.5 %copy-start.19 = (f32[128]{0:T(128)}, f32[128]{0:T(128)S(1)}, u32[]{:S(2)}) copy-start(f32[128]{0:T(128)S(1)} %add_rsqrt_fusion.1) | copy-start | bytes 1540
  262.4 4.1 %copy-start.28 = (bf16[1,2560,20]{1,2,0:T(8,128)(2,1)S(1)}, bf16[1,2560,20]{1,2,0:T(8,128)(2,1)}, u32[]{:S(2)}) copy-start(bf16[1,2560,20]{1,2,0:T(8,128)(2,1)} %param.24) | copy-start | bytes 307204
  262.4 4.1 %copy-start.30 = (f32[1,20]{1,0:T(1,128)S(1)}, f32[1,20]{1,0:T(1,128)}, u32[]{:S(2)}) copy-start(f32[1,20]{1,0:T(1,128)} %param.27) | copy-start | bytes 244
  267.4 4.8 %collective-permute-start.4 = (bf16[3,1536]{1,0:T(4,128)(2,1)S(1)}, bf16[3,1536]{1,0:T(4,128)(2,1)S(1)}, u32[]{:S(2)}, u32[]{:S(2)}) collective-permute-start(bf16[3,1536]{1,0:T(4,128)(2,1)S(1)} %pad_maximum_fusion.2), channel_id=1, source_target_pairs={{0,1},{1,2},{2,3},{4,5},{5,6},{6,7},{8,9},{9,10},{10,11},{12,13},{... | collective-permute-start | bytes 27656 | tf_op jit(solution)/shard_map/ppermute | solution.py:14
  274.1 79.6 %reduce-scatter.14.cloned.1.call-start = ((), (), s32[]{:S(2)}) async-start(), calls=%async_computation.9 | async-start | bytes 819200
  309.6 1.0 copy-start.14
  309.6 1.0 copy-start.33
  311.2 1.1 copy-start.3
  311.2 1.1 copy-start.20
  327.2 1.1 copy-start.7
Sparse Core Ops, SparseCore 0:
  8.9 20.8 all-gather.10
  48.8 33.3 all-gather.12
  101.4 25.1 reduce-scatter.9
  161.3 34.9 all-gather.14
  219.5 25.2 reduce-scatter.11
  274.2 35.2 all-gather.16
  328.5 25.1 reduce-scatter.13
where the time goes:
time: 364 us; the launch traced here: 362 us
  waiting for transfers between devices  167 us (46%)
  blocking collectives  66.3 us (18%)
  matrix products  51.1 us (14%)
  local copies, waits for them, and re-layouts  31.4 us (9%)
  starting transfers between devices  17.7 us (5%)
  other arithmetic  14.7 us (4%)
  between operations  14.3 us (4%)
    unnamed x10, waiting for transfers between devices  75.1 us
    all_gather x3, waiting for transfers between devices, prefix(): lax.all_gather(a.astype(kind), axis)  63.2 us
    all_gather x3, blocking collectives, prefix(): lax.all_gather(a.astype(kind), axis)  35 us
    all_gather x1, waiting for transfers between devices, shards(): all_tokens = lax.all_gather(tokens, 'tensor', axis=2, tiled=True)  20.2 us
    ppermute x5, starting transfers between devices, shifted(): lax.ppermute(value, axis, [(source, source + steps) for source in range(f...  17.5 us
    psum x3, blocking collectives, mixer(): squares = lax.psum(jnp.sum(gated * gated, axis=1), 'tensor')  17.5 us
    dot_general x3, matrix products, mixer(): jnp.dot(normed_in, gate_weight, preferred_element_type=jnp.float32)  14.9 us
    all_gather x2, blocking collectives, shards(): incoming = lax.all_gather(carried, 'tensor', axis=1, tiled=True)  13.8 us
  transfers between devices with their start and end apart: 12, of which 11 were waited for; matrix products, arithmetic and copies ran while one was open for 3% of the time, Pallas kernels for 0%

commit v1 on v0

--- a/solution.py
+++ b/solution.py
@@ -180,7 +180,14 @@
     section = lax.axis_index("pipe")
     share = lax.axis_size("tensor")
     member = lax.axis_index("tensor")
-    all_tokens = lax.all_gather(tokens, "tensor", axis=2, tiled=True)
+    ring = [tokens]
+    for hop_ in range(3):
+        ring.append(lax.ppermute(ring[-1], "tensor", [(dev, (dev + 1) % 4) for dev in range(4)]))
+    all_tokens = jnp.roll(
+        jnp.concatenate(ring[::-1], axis=2),
+        (lax.axis_index("tensor") + 1) * ring[0].shape[2],
+        axis=2,
+    )
     micro_count, rows, width = all_tokens.shape
     narrow = width // share
     outputs = jnp.zeros((micro_count, rows, narrow), jnp.bfloat16)

time: 364 us -> 350 us (0.962)
  local copies, waits for them, and re-layouts: 31.4 us -> 23.9 us
    all_gather x1 -> x0, waiting for transfers between devices: 20.2 us -> none  [shards(): all_tokens = lax.all_gather(tokens, 'tensor', axis=2, tiled=True)]
    ppermute x0 -> x3, waiting for transfers between devices: none -> 17.6 us  [shards(): lax.ppermute(ring[-1], 'tensor', [(dev, (dev + 1) % 4) for dev in range(4)])]
    unnamed x78 -> x71, local copies, waits for them, and re-layouts: 12.8 us -> 12 us
    unnamed x10 -> x9, waiting for transfers between devices: 75.1 us -> 75.3 us
  transfers between devices with their start and end apart: 12 -> 14, of which waited for: 11 -> 12; matrix products, arithmetic and copies ran while one was open for 3% -> 3% of each run, Pallas kernels for 0% -> 0%
where the time goes in v1:
time: 350 us; the launch traced here: 349 us
  waiting for transfers between devices  167 us (48%)
  blocking collectives  64 us (18%)
  matrix products  49 us (14%)
  local copies, waits for them, and re-layouts  23.9 us (7%)
  starting transfers between devices  18.7 us (5%)
  between operations  14.3 us (4%)
  other arithmetic  11.5 us (3%)
    unnamed x9, waiting for transfers between devices  75.3 us
    all_gather x3, waiting for transfers between devices, prefix(): lax.all_gather(a.astype(kind), axis)  66.5 us
    all_gather x3, blocking collectives, prefix(): lax.all_gather(a.astype(kind), axis)  32.7 us
    ppermute x5, starting transfers between devices, shifted(): lax.ppermute(value, axis, [(source, source + steps) for source in range(f...  17.9 us
    ppermute x3, waiting for transfers between devices, shards(): lax.ppermute(ring[-1], 'tensor', [(dev, (dev + 1) % 4) for dev in range(4)])  17.6 us
    psum x3, blocking collectives, mixer(): squares = lax.psum(jnp.sum(gated * gated, axis=1), 'tensor')  17.5 us
    dot_general x3, matrix products, mixer(): jnp.dot(normed_in, gate_weight, preferred_element_type=jnp.float32)  14.4 us
    all_gather x2, blocking collectives, shards(): incoming = lax.all_gather(carried, 'tensor', axis=1, tiled=True)  13.8 us
  transfers between devices with their start and end apart: 14, of which 12 were waited for; matrix products, arithmetic and copies ran while one was open for 3% of the time, Pallas kernels for 0%

profile of v1, /device:TPU:0, one launch (start us, length us, event | category | flops | bytes accessed | tf_op | source)
XLA Modules:
  0.0 348.7 jit_solution(3381046231970159478)
XLA Ops:
  7.0 6.9 %collective-permute-done = bf16[2,128,640]{2,1,0:T(8,128)(2,1)S(1)} collective-permute-done((bf16[2,128,640]{2,1,0:T(8,128)(2,1)}, bf16[2,128,640]{2,1,0:T(8,128)(2,1)S(1)}, u32[]{:S(2)}, u32[]{:S(2)}) %collective-permute-start) | collective-permute-done | bytes 327712 | tf_op jit(solution)/shard_map/ppermute | solution.py:185
  14.7 5.8 %collective-permute-done.1 = bf16[2,128,640]{2,1,0:T(8,128)(2,1)S(1)} collective-permute-done((bf16[2,128,640]{2,1,0:T(8,128)(2,1)S(1)}, bf16[2,128,640]{2,1,0:T(8,128)(2,1)S(1)}, u32[]{:S(2)}, u32[]{:S(2)}) %collective-permute-start.1) | collective-permute-done | bytes 327712 | tf_op jit(solution)/shard_map/ppermute | solution.py:185
  22.1 4.9 %collective-permute-done.2 = bf16[2,128,640]{2,1,0:T(8,128)(2,1)S(1)} collective-permute-done((bf16[2,128,640]{2,1,0:T(8,128)(2,1)S(1)}, bf16[2,128,640]{2,1,0:T(8,128)(2,1)S(1)}, u32[]{:S(2)}, u32[]{:S(2)}) %collective-permute-start.2) | collective-permute-done | bytes 327712 | tf_op jit(solution)/shard_map/ppermute | solution.py:185
  27.9 1.1 copy-done.1
  29.9 1.6 fusion.81
  31.5 4.2 %fusion.27 = bf16[128,1280]{1,0:T(8,128)(2,1)S(1)} fusion(bf16[1,2560,1280]{2,1,0:T(8,128)(2,1)} %param.22, f32[2560]{0:T(1024)S(1)} %reduce.3, f32[128]{0:T(128)S(1)} %add_rsqrt_fusion.5, bf16[2,128,5120]{2,1,0:T(8,128)(2,1)} %copy-done.1, s32[]{:T(128)S(6)} %select_n.106), kind=kOutput, calls=%fused_computation.27 | convolution fusion | flops 840335360 | bytes 7547396 | tf_op jit(solution)/shard_map/dot_general | solution.py:80
  35.8 4.2 %collective-permute-start.3 = (bf16[3,1536]{1,0:T(4,128)(2,1)S(1)}, bf16[3,1536]{1,0:T(4,128)(2,1)S(1)}, u32[]{:S(2)}, u32[]{:S(2)}) collective-permute-start(bf16[3,1536]{1,0:T(4,128)(2,1)S(1)} %pad_maximum_fusion), channel_id=1, source_target_pairs={{0,1},{1,2},{2,3},{4,5},{5,6},{6,7},{8,9},{9,10},{10,11},{12,13},{... | collective-permute-start | bytes 27656 | tf_op jit(solution)/shard_map/ppermute | solution.py:14
  43.4 11.9 %all-gather = bf16[4,1,20]{2,1,0:T(2,128)(2,1)S(1)} all-gather(bf16[1,1,20]{2,1,0:T(2,128)(2,1)S(1)} %get-tuple-element.257), channel_id=2, replica_groups=mesh['pipe'=2,'tensor'=4,'seq'=4] {'seq'}, dimensions={0}, use_global_device_ids=true | all-gather | bytes 200 | tf_op jit(solution)/shard_map/all_gather | solution.py:20
  55.9 22.1 %all-gather.10.cloned.1.call-done = bf16[80,64,128]{2,1,0:T(8,128)(2,1)} async-done(((bf16[20,64,128]{2,1,0:T(8,128)(2,1)}), bf16[80,64,128]{2,1,0:T(8,128)(2,1)}) %all-gather.10.cloned.1.call-update) | async-done | bytes 1310736 | tf_op jit(solution)/shard_map/all_gather | solution.py:20
  79.4 1.1 copy.76
  80.4 4.4 %multiply_reduce_fusion.2 = (f32[128]{0:T(128)S(1)}, f32[128,1280]{1,0:T(8,128)S(1)}) fusion(f32[128,1280]{1,0:T(8,128)} %copy.76, bf16[1,2560,1280]{2,1,0:T(8,128)(2,1)} %param.21, f32[2560]{0:T(1024)S(1)} %reduce.3, f32[128]{0:T(128)S(1)} %add_rsqrt_fusion.5, bf16[2,128,5120]{2,1,0:T(8,128)(2,1)} %copy-done.1, s32[]{:T(128)S(6)} %select_n.106), kind=kOutput, calls=%fused_computation.132 | convolution fusion | flops 841645952 | bytes 8530948 | tf_op jit(solution)/shard_map/dot_general | solution.py:77
  84.9 5.9 %psum.21 = f32[128]{0:T(128)S(1)} all-reduce(f32[128]{0:T(128)S(1)} %get-tuple-element.269), channel_id=1, replica_groups=mesh['pipe'=2,'tensor'=4,'seq'=4] {'tensor'}, use_global_device_ids=true, to_apply=%region_5.6 | all-reduce | flops 128 | bytes 1024 | tf_op jit(solution)/shard_map/psum | solution.py:145
  90.8 3.9 %fusion.18 = bf16[128,2560]{1,0:T(8,128)(2,1)S(1)} fusion(bf16[1,1280,2560]{2,1,0:T(8,128)(2,1)} %param.31, f32[128,1280]{1,0:T(8,128)S(1)} %get-tuple-element.270, f32[1280]{0:T(1024)S(1)} %reduce.7, f32[128]{0:T(128)S(1)} %add_rsqrt_fusion.4), kind=kOutput, calls=%fused_computation.24 | convolution fusion | flops 839680000 | bytes 7869952 | tf_op jit(solution)/shard_map/dot_general | solution.py:147
  94.7 1.1 copy.95
  95.9 25.3 %reduce-scatter.10.cloned.1.call-done = bf16[640,128]{1,0:T(8,128)(2,1)} async-done(((bf16[2560,128]{1,0:T(8,128)(2,1)}), bf16[640,128]{1,0:T(8,128)(2,1)}) %reduce-scatter.10.cloned.1.call-update) | async-done | bytes 163856
  121.2 1.1 copy.96
  122.3 1.1 bitcast_dynamic-update-slice_fusion.1
  123.4 3.4 collective-permute-start.4
  126.8 3.3 collective-permute-done.4
  130.0 6.9 %all_gather.32 = bf16[128,2560]{1,0:T(8,128)(2,1)S(1)} all-gather(bf16[128,640]{1,0:T(8,128)(2,1)S(1)} %collective-permute-done.4), channel_id=1, replica_groups=mesh['pipe'=2,'tensor'=4,'seq'=4] {'tensor'}, dimensions={1}, use_global_device_ids=true | all-gather | bytes 819200 | tf_op jit(solution)/shard_map/all_gather | solution.py:201
  136.9 1.6 fusion.57
  139.0 4.0 %fusion.30 = bf16[128,1280]{1,0:T(8,128)(2,1)S(1)} fusion(bf16[1,2560,1280]{2,1,0:T(8,128)(2,1)} %param.22, bf16[128,2560]{1,0:T(8,128)(2,1)S(1)} %get-tuple-element.247, f32[2560]{0:T(1024)S(1)} %reduce.3, f32[128]{0:T(128)S(1)} %add_rsqrt_fusion.3), kind=kOutput, calls=%fused_computation.28 | convolution fusion | flops 840335360 | bytes 7547392 | tf_op jit(solution)/shard_map/dot_general | solution.py:80
  144.4 3.6 %collective-permute-start.5 = (bf16[3,1536]{1,0:T(4,128)(2,1)S(1)}, bf16[3,1536]{1,0:T(4,128)(2,1)S(1)}, u32[]{:S(2)}, u32[]{:S(2)}) collective-permute-start(bf16[3,1536]{1,0:T(4,128)(2,1)S(1)} %pad_maximum_fusion.1), channel_id=1, source_target_pairs={{0,1},{1,2},{2,3},{4,5},{5,6},{6,7},{8,9},{9,10},{10,11},{12,13},{... | collective-permute-start | bytes 27656 | tf_op jit(solution)/shard_map/ppermute | solution.py:14
  148.6 1.1 copy.82
  152.5 10.3 %all-gather.2 = bf16[4,1,20]{2,1,0:T(2,128)(2,1)S(1)} all-gather(bf16[1,1,20]{2,1,0:T(2,128)(2,1)S(1)} %copy-done.17), channel_id=4, replica_groups=mesh['pipe'=2,'tensor'=4,'seq'=4] {'seq'}, dimensions={0}, use_global_device_ids=true | all-gather | bytes 200 | tf_op jit(solution)/shard_map/all_gather | solution.py:20
  164.3 22.2 %all-gather.12.cloned.1.call-done = bf16[80,64,128]{2,1,0:T(8,128)(2,1)} async-done(((bf16[20,64,128]{2,1,0:T(8,128)(2,1)}), bf16[80,64,128]{2,1,0:T(8,128)(2,1)}) %all-gather.12.cloned.1.call-update) | async-done | bytes 1310736 | tf_op jit(solution)/shard_map/all_gather | solution.py:20
  188.4 1.1 copy.85
  189.5 5.0 %multiply_reduce_fusion.1 = (f32[128]{0:T(128)S(1)}, f32[128,1280]{1,0:T(8,128)}) fusion(f32[128,1280]{1,0:T(8,128)} %copy.85, bf16[1,2560,1280]{2,1,0:T(8,128)(2,1)} %param.21, bf16[128,2560]{1,0:T(8,128)(2,1)S(1)} %get-tuple-element.247, f32[2560]{0:T(1024)S(1)} %reduce.3, f32[128]{0:T(128)S(1)} %copy-done.13), kind=kOutput, calls=%fused_computation.123 | convolution fusion | flops 841645952 | bytes 8530944 | tf_op jit(solution)/shard_map/dot_general | solution.py:77
  194.5 5.8 %psum.22 = f32[128]{0:T(128)S(1)} all-reduce(f32[128]{0:T(128)S(1)} %get-tuple-element.271), channel_id=1, replica_groups=mesh['pipe'=2,'tensor'=4,'seq'=4] {'tensor'}, use_global_device_ids=true, to_apply=%region_12.13 | all-reduce | flops 128 | bytes 1024 | tf_op jit(solution)/shard_map/psum | solution.py:145
  200.3 4.2 %fusion.21 = bf16[128,2560]{1,0:T(8,128)(2,1)S(1)} fusion(bf16[1,1280,2560]{2,1,0:T(8,128)(2,1)} %param.31, f32[128,1280]{1,0:T(8,128)} %get-tuple-element.272, f32[128]{0:T(128)S(1)} %add_rsqrt_fusion.2, f32[1280]{0:T(1024)S(1)} %reduce.7), kind=kOutput, calls=%fused_computation.25 | convolution fusion | flops 839680000 | bytes 7869952 | tf_op jit(solution)/shard_map/dot_general | solution.py:147
  204.5 1.1 copy.97
  205.7 25.3 %reduce-scatter.12.cloned.1.call-done = bf16[640,128]{1,0:T(8,128)(2,1)} async-done(((bf16[2560,128]{1,0:T(8,128)(2,1)}), bf16[640,128]{1,0:T(8,128)(2,1)}) %reduce-scatter.12.cloned.1.call-update) | async-done | bytes 163856
  231.0 1.1 copy.98
  232.1 3.4 collective-permute-start.6
  235.5 3.3 collective-permute-done.6
  238.8 6.9 %all_gather.35 = bf16[128,2560]{1,0:T(8,128)(2,1)S(1)} all-gather(bf16[128,640]{1,0:T(8,128)(2,1)S(1)} %collective-permute-done.6), channel_id=1, replica_groups=mesh['pipe'=2,'tensor'=4,'seq'=4] {'tensor'}, dimensions={1}, use_global_device_ids=true | all-gather | bytes 819200 | tf_op jit(solution)/shard_map/all_gather | solution.py:201
  245.7 1.6 fusion.60
  247.8 4.0 %fusion.33 = bf16[128,1280]{1,0:T(8,128)(2,1)S(1)} fusion(bf16[1,2560,1280]{2,1,0:T(8,128)(2,1)} %param.22, bf16[128,2560]{1,0:T(8,128)(2,1)S(1)} %get-tuple-element.241, f32[128]{0:T(128)S(1)} %add_rsqrt_fusion.1, f32[2560]{0:T(1024)S(1)} %reduce.3), kind=kOutput, calls=%fused_computation.29 | convolution fusion | flops 840335360 | bytes 7547392 | tf_op jit(solution)/shard_map/dot_general | solution.py:80
  253.2 3.4 collective-permute-start.7
  257.3 1.1 copy.91
  261.2 10.5 %all-gather.4 = bf16[4,1,20]{2,1,0:T(2,128)(2,1)S(1)} all-gather(bf16[1,1,20]{2,1,0:T(2,128)(2,1)S(1)} %copy-done.16), channel_id=6, replica_groups=mesh['pipe'=2,'tensor'=4,'seq'=4] {'seq'}, dimensions={0}, use_global_device_ids=true | all-gather | bytes 200 | tf_op jit(solution)/shard_map/all_gather | solution.py:20
  273.2 22.2 %all-gather.14.cloned.1.call-done = bf16[80,64,128]{2,1,0:T(8,128)(2,1)} async-done(((bf16[20,64,128]{2,1,0:T(8,128)(2,1)}), bf16[80,64,128]{2,1,0:T(8,128)(2,1)}) %all-gather.14.cloned.1.call-update) | async-done | bytes 1310736 | tf_op jit(solution)/shard_map/all_gather | solution.py:20
  297.5 1.1 copy.94
  298.5 5.0 %multiply_reduce_fusion = (f32[128]{0:T(128)S(1)}, f32[128,1280]{1,0:T(8,128)}) fusion(f32[128,1280]{1,0:T(8,128)} %copy.94, bf16[1,2560,1280]{2,1,0:T(8,128)(2,1)} %param.21, bf16[128,2560]{1,0:T(8,128)(2,1)S(1)} %get-tuple-element.241, f32[128]{0:T(128)S(1)} %copy-done.11, f32[2560]{0:T(1024)S(1)} %reduce.3), kind=kOutput, calls=%fused_computation.114 | convolution fusion | flops 841645952 | bytes 8530944 | tf_op jit(solution)/shard_map/dot_general | solution.py:77
  303.5 5.8 %psum.23 = f32[128]{0:T(128)S(1)} all-reduce(f32[128]{0:T(128)S(1)} %get-tuple-element.273), channel_id=1, replica_groups=mesh['pipe'=2,'tensor'=4,'seq'=4] {'tensor'}, use_global_device_ids=true, to_apply=%region_19.20 | all-reduce | flops 128 | bytes 1024 | tf_op jit(solution)/shard_map/psum | solution.py:145
  309.4 4.2 %fusion.24 = bf16[128,2560]{1,0:T(8,128)(2,1)S(1)} fusion(bf16[1,1280,2560]{2,1,0:T(8,128)(2,1)} %param.31, f32[128,1280]{1,0:T(8,128)} %get-tuple-element.274, f32[128]{0:T(128)S(1)} %add_rsqrt_fusion, f32[1280]{0:T(1024)S(1)} %reduce.7), kind=kOutput, calls=%fused_computation.26 | convolution fusion | flops 839680000 | bytes 7869952 | tf_op jit(solution)/shard_map/dot_general | solution.py:147
  313.5 1.1 copy.99
  315.4 24.6 %reduce-scatter.14.cloned.1.call-done = bf16[640,128]{1,0:T(8,128)(2,1)} async-done(((bf16[2560,128]{1,0:T(8,128)(2,1)}), bf16[640,128]{1,0:T(8,128)(2,1)}) %reduce-scatter.14.cloned.1.call-update) | async-done | bytes 163856
  (187 shorter events, 29.8 us)
Async XLA Ops:
  6.5 23.4 %copy-start = (bf16[1,2560,256]{2,1,0:T(8,128)(2,1)S(1)}, bf16[1,2560,256]{2,1,0:T(8,128)(2,1)}, u32[]{:S(2)}) copy-start(bf16[1,2560,256]{2,1,0:T(8,128)(2,1)} %param.23) | copy-start | bytes 3932164
  6.5 20.6 %copy-start.4 = (bf16[2,128,640]{2,1,0:T(8,128)(2,1)S(1)}, bf16[2,128,640]{2,1,0:T(8,128)(2,1)}, u32[]{:S(2)}) copy-start(bf16[2,128,640]{2,1,0:T(8,128)(2,1)} %param.19) | copy-start | bytes 983044
  6.5 71.4 %all-gather.10.cloned.1.call-start = ((), (), s32[]{:S(2)}) async-start(), calls=%async_computation.3 | async-start | bytes 1638400 | tf_op jit(solution)/shard_map/all_gather | solution.py:20
  6.5 7.4 %collective-permute-start = (bf16[2,128,640]{2,1,0:T(8,128)(2,1)}, bf16[2,128,640]{2,1,0:T(8,128)(2,1)S(1)}, u32[]{:S(2)}, u32[]{:S(2)}) collective-permute-start(bf16[2,128,640]{2,1,0:T(8,128)(2,1)} %param.19), channel_id=1, source_target_pairs={{0,4},{4,8},{8,12},{12,0},{1,5},{5,9},{9,13},{13,1},{2,6},{6,10},{... | collective-permute-start | bytes 983048 | tf_op jit(solution)/shard_map/ppermute | solution.py:185
  14.0 6.5 %collective-permute-start.1 = (bf16[2,128,640]{2,1,0:T(8,128)(2,1)S(1)}, bf16[2,128,640]{2,1,0:T(8,128)(2,1)S(1)}, u32[]{:S(2)}, u32[]{:S(2)}) collective-permute-start(bf16[2,128,640]{2,1,0:T(8,128)(2,1)S(1)} %collective-permute-done), channel_id=1, source_target_pairs={{0,4},{4,8},{8,12},{12,0},{1,5},{5,9},{9,13},{13,1},{2,6},{6,10},{... | collective-permute-start | bytes 983048 | tf_op jit(solution)/shard_map/ppermute | solution.py:185
  20.5 6.5 %collective-permute-start.2 = (bf16[2,128,640]{2,1,0:T(8,128)(2,1)S(1)}, bf16[2,128,640]{2,1,0:T(8,128)(2,1)S(1)}, u32[]{:S(2)}, u32[]{:S(2)}) collective-permute-start(bf16[2,128,640]{2,1,0:T(8,128)(2,1)S(1)} %collective-permute-done.1), channel_id=1, source_target_pairs={{0,4},{4,8},{8,12},{12,0},{1,5},{5,9},{9,13},{13,1},{2,6},{6,10},{... | collective-permute-start | bytes 983048 | tf_op jit(solution)/shard_map/ppermute | solution.py:185
  27.3 1.7 copy-start.18
  27.3 1.7 copy-start.21
  27.4 2.1 copy-start.8
  27.5 1.5 copy-start.1
  35.8 5.6 %collective-permute-start.3 = (bf16[3,1536]{1,0:T(4,128)(2,1)S(1)}, bf16[3,1536]{1,0:T(4,128)(2,1)S(1)}, u32[]{:S(2)}, u32[]{:S(2)}) collective-permute-start(bf16[3,1536]{1,0:T(4,128)(2,1)S(1)} %pad_maximum_fusion), channel_id=1, source_target_pairs={{0,1},{1,2},{2,3},{4,5},{5,6},{6,7},{8,9},{9,10},{10,11},{12,13},{... | collective-permute-start | bytes 27656 | tf_op jit(solution)/shard_map/ppermute | solution.py:14
  42.0 1.4 copy-start.7
  43.3 77.9 %reduce-scatter.10.cloned.1.call-start = ((), (), s32[]{:S(2)}) async-start(), calls=%async_computation.6 | async-start | bytes 819200
  78.0 0.7 copy-start.24
  95.8 90.7 %all-gather.12.cloned.1.call-start = ((), (), s32[]{:S(2)}) async-start(), calls=%async_computation.4 | async-start | bytes 1638400 | tf_op jit(solution)/shard_map/all_gather | solution.py:20
  123.4 6.7 %collective-permute-start.4 = (bf16[128,640]{1,0:T(8,128)(2,1)S(1)}, bf16[128,640]{1,0:T(8,128)(2,1)S(1)}, u32[]{:S(2)}, u32[]{:S(2)}) collective-permute-start(bf16[128,640]{1,0:T(8,128)(2,1)S(1)} %get-tuple-element.249), channel_id=1, source_target_pairs={{0,16},{1,17},{2,18},{3,19},{4,20},{5,21},{6,22},{7,23},{8,24},{9,... | collective-permute-start | bytes 491528 | tf_op jit(solution)/shard_map/ppermute | solution.py:14
  138.5 4.4 %copy-start.12 = (f32[128]{0:T(128)}, f32[128]{0:T(128)S(1)}, u32[]{:S(2)}) copy-start(f32[128]{0:T(128)S(1)} %add_rsqrt_fusion.3) | copy-start | bytes 1540
  139.0 4.0 %copy-start.19 = (bf16[1,2560,20]{1,2,0:T(8,128)(2,1)S(1)}, bf16[1,2560,20]{1,2,0:T(8,128)(2,1)}, u32[]{:S(2)}) copy-start(bf16[1,2560,20]{1,2,0:T(8,128)(2,1)} %param.24) | copy-start | bytes 307204
  139.0 4.0 %copy-start.22 = (f32[1,20]{1,0:T(1,128)S(1)}, f32[1,20]{1,0:T(1,128)}, u32[]{:S(2)}) copy-start(f32[1,20]{1,0:T(1,128)} %param.27) | copy-start | bytes 244
  144.4 5.3 %collective-permute-start.5 = (bf16[3,1536]{1,0:T(4,128)(2,1)S(1)}, bf16[3,1536]{1,0:T(4,128)(2,1)S(1)}, u32[]{:S(2)}, u32[]{:S(2)}) collective-permute-start(bf16[3,1536]{1,0:T(4,128)(2,1)S(1)} %pad_maximum_fusion.1), channel_id=1, source_target_pairs={{0,1},{1,2},{2,3},{4,5},{5,6},{6,7},{8,9},{9,10},{10,11},{12,13},{... | collective-permute-start | bytes 27656 | tf_op jit(solution)/shard_map/ppermute | solution.py:14
  149.7 1.1 copy-start.3
  150.8 0.7 copy-start.15
  151.3 1.3 copy-start.17
  152.5 78.5 %reduce-scatter.12.cloned.1.call-start = ((), (), s32[]{:S(2)}) async-start(), calls=%async_computation.7 | async-start | bytes 819200
  186.6 1.1 copy-start.6
  186.6 1.1 copy-start.25
  188.4 1.1 copy-start.13
  205.6 89.8 %all-gather.14.cloned.1.call-start = ((), (), s32[]{:S(2)}) async-start(), calls=%async_computation.5 | async-start | bytes 1638400 | tf_op jit(solution)/shard_map/all_gather | solution.py:20
  232.1 6.7 %collective-permute-start.6 = (bf16[128,640]{1,0:T(8,128)(2,1)S(1)}, bf16[128,640]{1,0:T(8,128)(2,1)S(1)}, u32[]{:S(2)}, u32[]{:S(2)}) collective-permute-start(bf16[128,640]{1,0:T(8,128)(2,1)S(1)} %get-tuple-element.243), channel_id=1, source_target_pairs={{0,16},{1,17},{2,18},{3,19},{4,20},{5,21},{6,22},{7,23},{8,24},{9,... | collective-permute-start | bytes 491528 | tf_op jit(solution)/shard_map/ppermute | solution.py:14
  247.3 4.4 %copy-start.10 = (f32[128]{0:T(128)}, f32[128]{0:T(128)S(1)}, u32[]{:S(2)}) copy-start(f32[128]{0:T(128)S(1)} %add_rsqrt_fusion.1) | copy-start | bytes 1540
  247.7 4.0 %copy-start.20 = (bf16[1,2560,20]{1,2,0:T(8,128)(2,1)S(1)}, bf16[1,2560,20]{1,2,0:T(8,128)(2,1)}, u32[]{:S(2)}) copy-start(bf16[1,2560,20]{1,2,0:T(8,128)(2,1)} %param.24) | copy-start | bytes 307204
  247.7 4.0 %copy-start.23 = (f32[1,20]{1,0:T(1,128)S(1)}, f32[1,20]{1,0:T(1,128)}, u32[]{:S(2)}) copy-start(f32[1,20]{1,0:T(1,128)} %param.27) | copy-start | bytes 244
  247.7 4.4 %copy-start.9 = (f32[1,20]{1,0:T(1,128)S(1)}, f32[1,20]{1,0:T(1,128)}, u32[]{:S(2)}) copy-start(f32[1,20]{1,0:T(1,128)} %param.28) | copy-start | bytes 244
  253.2 5.1 %collective-permute-start.7 = (bf16[3,1536]{1,0:T(4,128)(2,1)S(1)}, bf16[3,1536]{1,0:T(4,128)(2,1)S(1)}, u32[]{:S(2)}, u32[]{:S(2)}) collective-permute-start(bf16[3,1536]{1,0:T(4,128)(2,1)S(1)} %pad_maximum_fusion.2), channel_id=1, source_target_pairs={{0,1},{1,2},{2,3},{4,5},{5,6},{6,7},{8,9},{9,10},{10,11},{12,13},{... | collective-permute-start | bytes 27656 | tf_op jit(solution)/shard_map/ppermute | solution.py:14
  258.4 1.1 copy-start.2
  259.5 0.7 copy-start.14
  259.9 1.3 copy-start.16
  261.1 78.9 %reduce-scatter.14.cloned.1.call-start = ((), (), s32[]{:S(2)}) async-start(), calls=%async_computation.8 | async-start | bytes 819200
  295.7 1.1 copy-start.5
  295.7 1.1 copy-start.26
  297.5 1.1 copy-start.11
Sparse Core Ops, SparseCore 0:
  43.4 34.4 all-gather.9
  96.0 25.1 reduce-scatter.9
  152.6 33.8 all-gather.11
  205.7 25.1 reduce-scatter.11
  261.3 34.0 all-gather.13
  314.8 25.1 reduce-scatter.13
